TPU v7x, 256 devices: a whole 4x4x8 slice. The times are simulated.
256 devices in a mesh: expert: 64 (over x, z, core), pair: 2 (over y_lo), dp: 2 (over y_hi).
Axes of the slice: x: 4, y: 4 (y_hi: 2, y_lo: 2; y = y_hi * 2 + y_lo), z: 8, core: 2. Of those that a mesh axis runs over, the one named last changes fastest.
Arguments:
- tokens: bfloat16 [1024, 196, 768], P(('expert', 'pair', 'dp')), may hold values from -96 to 96
- phi: bfloat16 [768, 128], replicated, may hold values from -0.25 to 0.25
- w_in: bfloat16 [64, 768, 3072], P('expert', None, 'pair'), may hold values from -0.21875 to 0.21875
- w_out: bfloat16 [64, 3072, 768], P('expert', 'pair'), may hold values from -0.109375 to 0.109375
- slot_out: bfloat16 [1024, 128, 768], P(('expert', 'pair', 'dp')), may hold values from -6 to 6
- grad_out: bfloat16 [1024, 196, 768], P(('expert', 'pair', 'dp')), may hold values from -6 to 6
Outputs:
- token_grad: bfloat16 [1024, 196, 768], P(('expert', 'pair', 'dp'))
- phi_grad: float32 [768, 128], replicated
- grad_w_in: bfloat16 [64, 768, 3072], P('expert', 'dp', 'pair')
- grad_w_out: bfloat16 [64, 3072, 768], P('expert', 'pair', 'dp')
All inputs are finite; a program needn't handle non-finite values.
Results may differ from a plain program's by a relative error of at most 0.0086.
Values may be sent and summed in bfloat16 or wider, within the bound.
No kernel may reach another device: no remote copies, remote signals or barrier semaphores. Data moves between devices by JAX's collectives and lax.ppermute only.
A program may use at most 128 MiB of HBM per device.

v0:
```python
import jax
import jax.numpy as jnp
from jax import lax
from jax.sharding import PartitionSpec as P


def in_blocks(array, dim, peers):
    dims = array.shape
    pieces = array.reshape(*dims[:dim], peers, dims[dim] // peers, *dims[dim + 1 :])
    return jnp.moveaxis(pieces, dim, 0)


def sum_at_owner(array, axis, dim):
    pieces = in_blocks(array, dim, lax.axis_size(axis))
    arrived = lax.all_to_all(pieces, axis, split_axis=0, concat_axis=0, tiled=True)
    return arrived.sum(axis=0)


def summed_on_arrival(array, axis, dim):
    peers = lax.axis_size(axis)
    pieces = lax.all_to_all(in_blocks(array, dim, peers), axis, 0, 0, tiled=True)
    return jnp.sum(pieces.astype(jnp.float32), axis=0)


def expert_rows(z_rows, g_rows, w_first, w_second):
    pre = jnp.dot(z_rows, w_first, preferred_element_type=jnp.float32)
    act_full, gelu_back = jax.vjp(jax.nn.gelu, pre)
    act = act_full.astype(jnp.bfloat16)
    dact = lax.dot_general(
        g_rows, w_second, (((1,), (1,)), ((), ())), preferred_element_type=jnp.float32
    )
    dpre = gelu_back(dact)[0].astype(jnp.bfloat16)
    grad_second = lax.dot_general(
        act, g_rows, (((0,), (0,)), ((), ())), preferred_element_type=jnp.float32
    )
    grad_first = lax.dot_general(
        z_rows, dpre, (((0,), (0,)), ((), ())), preferred_element_type=jnp.float32
    )
    back = lax.dot_general(
        dpre, w_first, (((1,), (1,)), ((), ())), preferred_element_type=jnp.float32
    )
    return (grad_first, grad_second, back)


def local(tokens, phi, w_in, w_out, slot_out, grad_out):
    f32 = jnp.float32
    images, _, width = tokens.shape
    groups = lax.axis_size("expert")
    per_group = phi.shape[1] // groups
    experts_here = w_in.shape[0]
    slots = per_group // experts_here
    logits = jnp.einsum("bmd,ds->bms", tokens, phi, preferred_element_type=f32)
    dispatch = jax.nn.softmax(logits, axis=1)
    combine = jax.nn.softmax(logits, axis=2)
    dispatch_low = dispatch.astype(jnp.bfloat16)
    combine_low = combine.astype(jnp.bfloat16)
    slot_in = jnp.einsum("bms,bmd->bsd", dispatch_low, tokens, preferred_element_type=f32).astype(
        jnp.bfloat16
    )
    slot_grad = jnp.einsum(
        "bms,bmd->bsd", combine_low, grad_out, preferred_element_type=f32
    ).astype(jnp.bfloat16)
    outgoing_in = slot_in.reshape(images, groups, per_group, width)
    outgoing_grad = slot_grad.reshape(images, groups, per_group, width)
    arrived_in, arrived_grad = (
        lax.all_to_all(outgoing_in, "expert", split_axis=1, concat_axis=0, tiled=True),
        lax.all_to_all(outgoing_grad, "expert", split_axis=1, concat_axis=0, tiled=True),
    )
    rows_in, rows_grad = (
        lax.all_gather(arrived_in, "pair", axis=0, tiled=True),
        lax.all_gather(arrived_grad, "pair", axis=0, tiled=True),
    )
    count = rows_in.shape[0]
    z_rows = rows_in[:, 0].reshape(count * slots, width)
    g_rows = rows_grad[:, 0].reshape(count * slots, width)
    grad_first, grad_second, back = expert_rows(z_rows, g_rows, w_in[0], w_out[0])
    firsts = [grad_first]
    seconds = [grad_second]
    backs = back.reshape(count, 1, slots, width)
    back_sum = sum_at_owner(backs, "pair", 0)
    grad_w_in = lax.psum_scatter(
        jnp.stack(firsts).astype(jnp.bfloat16), "dp", scatter_dimension=1, tiled=True
    )
    grad_w_out = summed_on_arrival(jnp.stack(seconds).astype(jnp.bfloat16), "dp", 2).astype(
        jnp.bfloat16
    )
    back_low = back_sum.astype(jnp.bfloat16)
    returned = lax.all_to_all(back_low, "expert", split_axis=0, concat_axis=1, tiled=True)
    slot_in_grad = returned.reshape(images, groups * per_group, width)
    dispatch_grad = jnp.einsum("bmd,bsd->bms", tokens, slot_in_grad, preferred_element_type=f32)
    combine_grad = jnp.einsum("bmd,bsd->bms", grad_out, slot_out, preferred_element_type=f32)
    logit_grad = dispatch * (
        dispatch_grad - jnp.sum(dispatch * dispatch_grad, axis=1, keepdims=True)
    )
    logit_grad = logit_grad + combine * (
        combine_grad - jnp.sum(combine * combine_grad, axis=2, keepdims=True)
    )
    logit_low = logit_grad.astype(jnp.bfloat16)
    token_part = jnp.einsum("bms,bsd->bmd", dispatch_low, slot_in_grad, preferred_element_type=f32)
    token_grad = (
        token_part + jnp.einsum("bms,ds->bmd", logit_low, phi, preferred_element_type=f32)
    ).astype(jnp.bfloat16)
    phi_part = jnp.einsum("bmd,bms->ds", tokens, logit_low, preferred_element_type=f32)
    phi_grad = lax.psum(phi_part, ("expert", "pair", "dp"))
    return (token_grad, phi_grad, grad_w_in, grad_w_out)


def solution(mesh):
    in_specs = (
        P(("expert", "pair", "dp"), None, None),
        P(),
        P("expert", None, "pair"),
        P("expert", "pair", None),
        P(("expert", "pair", "dp"), None, None),
        P(("expert", "pair", "dp"), None, None),
    )
    out_specs = (
        P(("expert", "pair", "dp"), None, None),
        P(),
        P("expert", "dp", "pair"),
        P("expert", "pair", "dp"),
    )
    return jax.shard_map(local, mesh=mesh, in_specs=in_specs, out_specs=out_specs, check_vma=False)
```

profile of v0, /device:TPU:1, one launch (start us, length us, event | category | flops | bytes accessed | tf_op | source)
XLA Modules:
  0.0 530.7 jit_solution(16438834560802032734)
XLA Ops:
  16.8 13.0 %all-to-all-start.1 = ((bf16[4,64,2,768]{3,2,0,1:T(2,128)(2,1)}), bf16[4,64,2,768]{3,2,0,1:T(2,128)(2,1)S(1)}, u32[]{:S(2)}, u32[]{:S(2)}) async-start(bf16[4,64,2,768]{3,2,0,1:T(2,128)(2,1)} %copy.36), calls=%async_computation.1 | async-start | bytes 1572864 | tf_op jit(solution)/shard_map/all_to_all | solution.py:66
  31.4 21.3 %all-to-all-done.1 = bf16[4,64,2,768]{3,2,0,1:T(2,128)(2,1)S(1)} async-done(((bf16[4,64,2,768]{3,2,0,1:T(2,128)(2,1)}), bf16[4,64,2,768]{3,2,0,1:T(2,128)(2,1)S(1)}, u32[]{:S(2)}, u32[]{:S(2)}) %all-to-all-start.1) | async-done | bytes 786464 | tf_op jit(solution)/shard_map/all_to_all | solution.py:66
  53.7 3.9 convolution_convert_fusion.3
  60.3 29.1 %all_to_all.61 = bf16[4,64,2,768]{3,2,0,1:T(2,128)(2,1)} all-to-all(bf16[4,64,2,768]{3,2,0,1:T(2,128)(2,1)S(1)} %copy.33), channel_id=1, replica_groups=mesh['expert'=64,'pair'=2,'dp'=2] {'expert'}, dimensions={1} | all-to-all | bytes 1572864 | tf_op jit(solution)/shard_map/all_to_all | solution.py:67
  89.4 4.6 reshape_squeeze.7
  94.1 5.9 %fusion.18 = f32[1024,1536]{1,0:T(8,128)} fusion(bf16[1024,768]{1,0:T(8,128)(2,1)} %reshape_squeeze.7, bf16[1,768,1536]{2,1,0:T(8,128)(2,1)S(1)} %copy-done), kind=kOutput, calls=%fused_computation.26 | convolution fusion | flops 2415919104 | bytes 10223616 | tf_op jit(solution)/shard_map/dot_general | solution.py:26
  100.0 18.7 %all-gather.3.cloned.1.call-done = bf16[512,1,2,768]{3,2,1,0:T(2,128)(2,1)} async-done(((bf16[256,1,2,768]{3,2,1,0:T(2,128)(2,1)}), bf16[512,1,2,768]{3,2,1,0:T(2,128)(2,1)}) %all-gather.3.cloned.1.call-update) | async-done | bytes 1572880 | tf_op jit(solution)/shard_map/all_gather | solution.py:71
  118.7 4.7 reshape_squeeze.6
  123.4 9.6 %fusion.10 = bf16[1024,1536]{1,0:T(8,128)(2,1)} fusion(f32[1024,1536]{1,0:T(8,128)} %fusion.18, bf16[1024,768]{1,0:T(8,128)(2,1)} %reshape_squeeze.6, bf16[1,1536,768]{2,1,0:T(8,128)(2,1)} %param.9), kind=kOutput, calls=%fused_computation.12 | convolution fusion | flops 2447376384 | bytes 13369344 | tf_op jit(solution)/shard_map/dot_general | solution.py:29
  133.0 7.2 %reshape.49 = bf16[2,256,2,1536]{3,2,1,0:T(2,128)(2,1)} reshape(bf16[1024,1536]{1,0:T(8,128)(2,1)} %fusion.10) | data formatting | bytes 6291456 | tf_op jit(solution)/shard_map/reshape.20
  140.2 4.5 fusion.24
  144.7 38.0 %all_to_all.62 = f32[2,256,1,2,768]{4,1,3,2,0:T(8,128)S(1)} all-to-all(f32[2,256,1,2,768]{4,1,3,2,0:T(8,128)S(1)} %fusion.24), channel_id=1, replica_groups=mesh['expert'=64,'pair'=2,'dp'=2] {'pair'}, dimensions={0} | all-to-all | bytes 6291456 | tf_op jit(solution)/shard_map/all_to_all | solution.py:15
  184.6 11.7 %all-to-all-start.3 = ((bf16[256,1,2,768]{3,2,1,0:T(2,128)(2,1)}), bf16[256,1,2,768]{3,2,1,0:T(2,128)(2,1)S(1)}, u32[]{:S(2)}, u32[]{:S(2)}) async-start(bf16[256,1,2,768]{3,2,1,0:T(2,128)(2,1)} %copy.41), calls=%async_computation.3 | async-start | bytes 1572864 | tf_op jit(solution)/shard_map/all_to_all | solution.py:88
  196.3 2.7 fusion.39
  199.1 20.1 %all-to-all-done.3 = bf16[256,1,2,768]{3,2,1,0:T(2,128)(2,1)S(1)} async-done(((bf16[256,1,2,768]{3,2,1,0:T(2,128)(2,1)}), bf16[256,1,2,768]{3,2,1,0:T(2,128)(2,1)S(1)}, u32[]{:S(2)}, u32[]{:S(2)}) %all-to-all-start.3) | async-done | bytes 786464 | tf_op jit(solution)/shard_map/all_to_all | solution.py:88
  225.9 6.8 %convolution_bitcast_fusion.1 = f32[768,128]{0,1:T(8,128)} fusion(f32[4,196,128]{2,1,0:T(8,128)} %fusion.37, f32[4,196,128]{2,1,0:T(8,128)} %fusion.39, bf16[4,196,768]{2,0,1:T(4,128)(2,1)} %param.6, f32[4,196,128]{2,1,0:T(8,128)} %get-tuple-element.19, f32[4,196]{1,0:T(4,128)} %get-tuple-element.18), kind=kOutput, calls=%fused_computation.43 | convolution fusion | flops 154844048 | bytes 2804800 | tf_op jit(solution)/shard_map/bmd,bms->ds/dot_general | solution.py:103
  232.8 6.4 %fusion.16 = bf16[1,768,1536]{2,1,0:T(8,128)(2,1)} fusion(bf16[1024,768]{1,0:T(8,128)(2,1)} %reshape_squeeze.7, bf16[1024,1536]{1,0:T(8,128)(2,1)} %fusion.10), kind=kOutput, calls=%fused_computation.22 | convolution fusion | flops 2417098752 | bytes 7077888 | tf_op jit(solution)/shard_map/dot_general | solution.py:36
  239.2 6.2 %convolution_convert_fusion = bf16[1536,768]{0,1:T(8,128)(2,1)S(1)} fusion(bf16[1024,768]{1,0:T(8,128)(2,1)} %reshape_squeeze.6, f32[1024,1536]{1,0:T(8,128)} %fusion.18), kind=kOutput, calls=%fused_computation.14 | convolution fusion | flops 2431254528 | bytes 10223616 | tf_op jit(solution)/shard_map/dot_general | solution.py:33
  245.4 32.5 %all_to_all.63 = bf16[2,1,1536,384]{2,3,1,0:T(8,128)(2,1)S(1)} all-to-all(bf16[2,1,1536,384]{2,3,1,0:T(8,128)(2,1)S(1)} %bitcast.83), channel_id=1, replica_groups=mesh['expert'=64,'pair'=2,'dp'=2] {'dp'}, dimensions={0} | all-to-all | bytes 4718592 | tf_op jit(solution)/shard_map/all_to_all | solution.py:21
  279.7 6.9 %fusion.42 = f32[4,196,768]{2,1,0:T(8,128)} fusion(f32[4,196,128]{2,1,0:T(8,128)} %fusion.37, f32[4,196,128]{2,1,0:T(8,128)} %fusion.39, bf16[768,128]{1,0:T(8,128)(2,1)} %param.7, f32[4,196,128]{2,1,0:T(8,128)} %get-tuple-element.19, f32[4,196]{1,0:T(4,128)S(1)} %copy-done.6), kind=kOutput, calls=%fused_computation.48 | convolution fusion | flops 154844048 | bytes 3812416 | tf_op jit(solution)/shard_map/bms,ds->bmd/dot_general | solution.py:101
  286.6 3.5 add_convert_fusion
  290.2 2.8 copy.48
  292.9 188.6 %all-reduce.2.cloned.1.call-done = f32[768,128]{0,1:T(8,128)} async-done(((f32[768,128]{0,1:T(8,128)}), f32[768,128]{0,1:T(8,128)}) %all-reduce.2.cloned.1.call-update) | async-done | bytes 393232 | tf_op jit(solution)/shard_map/psum | solution.py:104
  483.5 40.7 %reduce-scatter.2.cloned.1.call-done = bf16[1,384,1536]{2,1,0:T(8,128)(2,1)} async-done(((bf16[1,768,1536]{2,1,0:T(8,128)(2,1)}), bf16[1,384,1536]{2,1,0:T(8,128)(2,1)}) %reduce-scatter.2.cloned.1.call-update) | async-done | bytes 1179664 | tf_op jit(solution)/shard_map/reduce_scatter | solution.py:81
  (46 shorter events, 27.3 us)
Async XLA Ops:
  7.2 86.9 %copy-start = (bf16[1,768,1536]{2,1,0:T(8,128)(2,1)S(1)}, bf16[1,768,1536]{2,1,0:T(8,128)(2,1)}, u32[]{:S(2)}) copy-start(bf16[1,768,1536]{2,1,0:T(8,128)(2,1)} %param.8) | copy-start | bytes 7077892
  9.1 44.6 %copy-start.4 = (f32[4,196,128]{2,1,0:T(8,128)}, f32[4,196,128]{2,1,0:T(8,128)S(1)}, u32[]{:S(2)}) copy-start(f32[4,196,128]{2,1,0:T(8,128)S(1)} %fusion.46) | copy-start | bytes 1204228
  10.0 0.6 copy-start.7
  16.8 35.9 %all-to-all-start.1 = ((bf16[4,64,2,768]{3,2,0,1:T(2,128)(2,1)}), bf16[4,64,2,768]{3,2,0,1:T(2,128)(2,1)S(1)}, u32[]{:S(2)}, u32[]{:S(2)}) async-start(bf16[4,64,2,768]{3,2,0,1:T(2,128)(2,1)} %copy.36), calls=%async_computation.1 | async-start | bytes 1572864 | tf_op jit(solution)/shard_map/all_to_all | solution.py:66
  29.8 59.6 %all-gather.5.cloned.1.call-start = ((), (), s32[]{:S(2)}) async-start(), calls=%async_computation.7 | async-start | bytes 2359296 | tf_op jit(solution)/shard_map/all_gather | solution.py:70
  52.7 0.9 copy-start.1
  53.6 65.0 %all-gather.3.cloned.1.call-start = ((), (), s32[]{:S(2)}) async-start(), calls=%async_computation.6 | async-start | bytes 2359296 | tf_op jit(solution)/shard_map/all_gather | solution.py:71
  184.6 34.6 %all-to-all-start.3 = ((bf16[256,1,2,768]{3,2,1,0:T(2,128)(2,1)}), bf16[256,1,2,768]{3,2,1,0:T(2,128)(2,1)S(1)}, u32[]{:S(2)}, u32[]{:S(2)}) async-start(bf16[256,1,2,768]{3,2,1,0:T(2,128)(2,1)} %copy.41), calls=%async_computation.3 | async-start | bytes 1572864 | tf_op jit(solution)/shard_map/all_to_all | solution.py:88
  196.3 285.3 %all-reduce.2.cloned.1.call-start = ((), (), s32[]{:S(2)}) async-start(), calls=%async_computation.8 | async-start | bytes 786432 | tf_op jit(solution)/shard_map/psum | solution.py:104
  220.6 4.4 copy-start.5
  222.9 3.0 copy-start.2
  222.9 2.1 copy-start.8
  232.8 291.4 %reduce-scatter.2.cloned.1.call-start = ((), (), s32[]{:S(2)}) async-start(), calls=%async_computation.9 | async-start | bytes 3538944 | tf_op jit(solution)/shard_map/reduce_scatter | solution.py:81
  277.9 1.8 copy-start.6
  278.3 8.4 %copy-start.9 = (f32[4,128]{1,0:T(4,128)S(1)}, f32[4,128]{1,0:T(4,128)}, u32[]{:S(2)}) copy-start(f32[4,128]{1,0:T(4,128)} %copy-done.7) | copy-start | bytes 6148
  279.7 6.9 %copy-start.3 = (bf16[4,128,768]{2,1,0:T(8,128)(2,1)S(1)}, bf16[4,128,768]{2,1,0:T(8,128)(2,1)}, u32[]{:S(2)}) copy-start(bf16[4,128,768]{2,1,0:T(8,128)(2,1)} %copy-done.2) | copy-start | bytes 2359300
Sparse Core Ops, SparseCore 0:
  53.8 29.1 all-gather.4
  89.5 29.1 all-gather.2
  232.9 248.6 all-reduce.1
  484.5 39.6 reduce-scatter.1
where the time goes:
time: 532 us; the launch traced here: 531 us
  waiting for transfers between devices  290 us (55%)
  blocking collectives  99.5 us (19%)
  matrix products  63.2 us (12%)
  local copies, waits for them, and re-layouts  35.8 us (7%)
  starting transfers between devices  24.8 us (5%)
  between operations  13.9 us (3%)
    psum x1, waiting for transfers between devices, local(): phi_grad = lax.psum(phi_part, ('expert', 'pair', 'dp'))  189 us
    reduce_scatter x1, waiting for transfers between devices, local(): lax.psum_scatter(jnp.stack(firsts).astype(jnp.bfloat16), 'dp', scatter_di...  40.7 us
    all_to_all x1, blocking collectives, sum_at_owner(): lax.all_to_all(pieces, axis, split_axis=0, concat_axis=0, tiled=True)  38 us
    all_to_all x1, blocking collectives, summed_on_arrival(): lax.all_to_all(in_blocks(array, dim, peers), axis, 0, 0, tiled=True)  32.5 us
    all_to_all x1, blocking collectives, local(): lax.all_to_all(outgoing_grad, 'expert', split_axis=1, concat_axis=0, tile...  29.1 us
    all_to_all x1, waiting for transfers between devices, local(): lax.all_to_all(outgoing_in, 'expert', split_axis=1, concat_axis=0, tiled=...  21.3 us
    all_to_all x1, waiting for transfers between devices, local(): lax.all_to_all(back_low, 'expert', split_axis=0, concat_axis=1, tiled=True)  20.1 us
    all_gather x1, waiting for transfers between devices, local(): lax.all_gather(arrived_grad, 'pair', axis=0, tiled=True)  18.7 us
  transfers between devices with their start and end apart: 6, of which 5 were waited for; matrix products, arithmetic and copies ran while one was open for 10% of the time, Pallas kernels for 0%

commit v1 on v0

--- a/solution.py
+++ b/solution.py
@@ -101,7 +101,7 @@
         token_part + jnp.einsum("bms,ds->bmd", logit_low, phi, preferred_element_type=f32)
     ).astype(jnp.bfloat16)
     phi_part = jnp.einsum("bmd,bms->ds", tokens, logit_low, preferred_element_type=f32)
-    phi_grad = lax.psum(phi_part, ("expert", "pair", "dp"))
+    phi_grad = lax.psum(lax.psum(phi_part, ("pair", "dp")), "expert")
     return (token_grad, phi_grad, grad_w_in, grad_w_out)
 
 

time: 532 us -> 514 us (0.966)
  waiting for transfers between devices: 290 us -> 275 us
    psum x1 -> x2, waiting for transfers between devices: 189 us -> 172 us  [local(): phi_grad = lax.psum(lax.psum(phi_part, ('pair', 'dp')), 'expert')]
  transfers between devices with their start and end apart: 6 -> 7, of which waited for: 5 -> 6; matrix products, arithmetic and copies ran while one was open for 10% -> 10% of each run, Pallas kernels for 0% -> 0%
where the time goes in v1:
time: 514 us; the launch traced here: 513 us
  waiting for transfers between devices  275 us (54%)
  blocking collectives  96.6 us (19%)
  matrix products  63.1 us (12%)
  local copies, waits for them, and re-layouts  35.8 us (7%)
  starting transfers between devices  24.9 us (5%)
  between operations  13.9 us (3%)
    psum x2, waiting for transfers between devices, local(): phi_grad = lax.psum(lax.psum(phi_part, ('pair', 'dp')), 'expert')  172 us
    reduce_scatter x1, waiting for transfers between devices, local(): lax.psum_scatter(jnp.stack(firsts).astype(jnp.bfloat16), 'dp', scatter_di...  42.7 us
    all_to_all x1, blocking collectives, sum_at_owner(): lax.all_to_all(pieces, axis, split_axis=0, concat_axis=0, tiled=True)  38 us
    all_to_all x1, blocking collectives, summed_on_arrival(): lax.all_to_all(in_blocks(array, dim, peers), axis, 0, 0, tiled=True)  29.6 us
    all_to_all x1, blocking collectives, local(): lax.all_to_all(outgoing_grad, 'expert', split_axis=1, concat_axis=0, tile...  29.1 us
    all_to_all x1, waiting for transfers between devices, local(): lax.all_to_all(outgoing_in, 'expert', split_axis=1, concat_axis=0, tiled=...  21.3 us
    all_to_all x1, waiting for transfers between devices, local(): lax.all_to_all(back_low, 'expert', split_axis=0, concat_axis=1, tiled=True)  20.1 us
    all_gather x1, waiting for transfers between devices, local(): lax.all_gather(arrived_grad, 'pair', axis=0, tiled=True)  18.7 us
  transfers between devices with their start and end apart: 7, of which 6 were waited for; matrix products, arithmetic and copies ran while one was open for 10% of the time, Pallas kernels for 0%

profile of v1, /device:TPU:1, one launch (start us, length us, event | category | flops | bytes accessed | tf_op | source)
XLA Modules:
  0.0 513.4 jit_solution(12493824045756796472)
XLA Ops:
  16.8 13.0 %all-to-all-start.1 = ((bf16[4,64,2,768]{3,2,0,1:T(2,128)(2,1)}), bf16[4,64,2,768]{3,2,0,1:T(2,128)(2,1)S(1)}, u32[]{:S(2)}, u32[]{:S(2)}) async-start(bf16[4,64,2,768]{3,2,0,1:T(2,128)(2,1)} %copy.36), calls=%async_computation.1 | async-start | bytes 1572864 | tf_op jit(solution)/shard_map/all_to_all | solution.py:66
  31.4 21.3 %all-to-all-done.1 = bf16[4,64,2,768]{3,2,0,1:T(2,128)(2,1)S(1)} async-done(((bf16[4,64,2,768]{3,2,0,1:T(2,128)(2,1)}), bf16[4,64,2,768]{3,2,0,1:T(2,128)(2,1)S(1)}, u32[]{:S(2)}, u32[]{:S(2)}) %all-to-all-start.1) | async-done | bytes 786464 | tf_op jit(solution)/shard_map/all_to_all | solution.py:66
  53.7 3.9 convolution_convert_fusion.3
  60.3 29.1 %all_to_all.61 = bf16[4,64,2,768]{3,2,0,1:T(2,128)(2,1)} all-to-all(bf16[4,64,2,768]{3,2,0,1:T(2,128)(2,1)S(1)} %copy.33), channel_id=1, replica_groups=mesh['expert'=64,'pair'=2,'dp'=2] {'expert'}, dimensions={1} | all-to-all | bytes 1572864 | tf_op jit(solution)/shard_map/all_to_all | solution.py:67
  89.4 4.6 reshape_squeeze.7
  94.1 5.9 %fusion.18 = f32[1024,1536]{1,0:T(8,128)} fusion(bf16[1024,768]{1,0:T(8,128)(2,1)} %reshape_squeeze.7, bf16[1,768,1536]{2,1,0:T(8,128)(2,1)S(1)} %copy-done), kind=kOutput, calls=%fused_computation.26 | convolution fusion | flops 2415919104 | bytes 10223616 | tf_op jit(solution)/shard_map/dot_general | solution.py:26
  100.0 18.7 %all-gather.3.cloned.1.call-done = bf16[512,1,2,768]{3,2,1,0:T(2,128)(2,1)} async-done(((bf16[256,1,2,768]{3,2,1,0:T(2,128)(2,1)}), bf16[512,1,2,768]{3,2,1,0:T(2,128)(2,1)}) %all-gather.3.cloned.1.call-update) | async-done | bytes 1572880 | tf_op jit(solution)/shard_map/all_gather | solution.py:71
  118.7 4.7 reshape_squeeze.6
  123.4 9.6 %fusion.10 = bf16[1024,1536]{1,0:T(8,128)(2,1)} fusion(f32[1024,1536]{1,0:T(8,128)} %fusion.18, bf16[1024,768]{1,0:T(8,128)(2,1)} %reshape_squeeze.6, bf16[1,1536,768]{2,1,0:T(8,128)(2,1)} %param.9), kind=kOutput, calls=%fused_computation.12 | convolution fusion | flops 2447376384 | bytes 13369344 | tf_op jit(solution)/shard_map/dot_general | solution.py:29
  133.0 7.2 %reshape.49 = bf16[2,256,2,1536]{3,2,1,0:T(2,128)(2,1)} reshape(bf16[1024,1536]{1,0:T(8,128)(2,1)} %fusion.10) | data formatting | bytes 6291456 | tf_op jit(solution)/shard_map/reshape.20
  140.2 4.5 fusion.24
  144.7 38.0 %all_to_all.62 = f32[2,256,1,2,768]{4,1,3,2,0:T(8,128)S(1)} all-to-all(f32[2,256,1,2,768]{4,1,3,2,0:T(8,128)S(1)} %fusion.24), channel_id=1, replica_groups=mesh['expert'=64,'pair'=2,'dp'=2] {'pair'}, dimensions={0} | all-to-all | bytes 6291456 | tf_op jit(solution)/shard_map/all_to_all | solution.py:15
  184.6 11.7 %all-to-all-start.3 = ((bf16[256,1,2,768]{3,2,1,0:T(2,128)(2,1)}), bf16[256,1,2,768]{3,2,1,0:T(2,128)(2,1)S(1)}, u32[]{:S(2)}, u32[]{:S(2)}) async-start(bf16[256,1,2,768]{3,2,1,0:T(2,128)(2,1)} %copy.41), calls=%async_computation.3 | async-start | bytes 1572864 | tf_op jit(solution)/shard_map/all_to_all | solution.py:88
  199.1 20.1 %all-to-all-done.3 = bf16[256,1,2,768]{3,2,1,0:T(2,128)(2,1)S(1)} async-done(((bf16[256,1,2,768]{3,2,1,0:T(2,128)(2,1)}), bf16[256,1,2,768]{3,2,1,0:T(2,128)(2,1)S(1)}, u32[]{:S(2)}, u32[]{:S(2)}) %all-to-all-start.3) | async-done | bytes 786464 | tf_op jit(solution)/shard_map/all_to_all | solution.py:88
  225.9 6.8 %convolution_bitcast_fusion.1 = f32[768,128]{0,1:T(8,128)} fusion(f32[4,196,128]{2,1,0:T(8,128)} %fusion.37, f32[4,196,128]{2,1,0:T(8,128)} %fusion.39, bf16[4,196,768]{2,0,1:T(4,128)(2,1)} %param.6, f32[4,196,128]{2,1,0:T(8,128)} %get-tuple-element.19, f32[4,196]{1,0:T(4,128)} %get-tuple-element.18), kind=kOutput, calls=%fused_computation.43 | convolution fusion | flops 154844048 | bytes 2804800 | tf_op jit(solution)/shard_map/bmd,bms->ds/dot_general | solution.py:103
  232.8 41.9 %all-reduce.3.cloned.1.call-done = f32[768,128]{0,1:T(8,128)} async-done(((f32[768,128]{0,1:T(8,128)}), f32[768,128]{0,1:T(8,128)}) %all-reduce.3.cloned.1.call-update) | async-done | bytes 393232 | tf_op jit(solution)/shard_map/psum | solution.py:104
  274.8 6.4 %fusion.16 = bf16[1,768,1536]{2,1,0:T(8,128)(2,1)} fusion(bf16[1024,768]{1,0:T(8,128)(2,1)} %reshape_squeeze.7, bf16[1024,1536]{1,0:T(8,128)(2,1)} %fusion.10), kind=kOutput, calls=%fused_computation.22 | convolution fusion | flops 2417098752 | bytes 7077888 | tf_op jit(solution)/shard_map/dot_general | solution.py:36
  281.3 6.1 %convolution_convert_fusion = bf16[1536,768]{0,1:T(8,128)(2,1)S(1)} fusion(bf16[1024,768]{1,0:T(8,128)(2,1)} %reshape_squeeze.6, f32[1024,1536]{1,0:T(8,128)} %fusion.18), kind=kOutput, calls=%fused_computation.14 | convolution fusion | flops 2431254528 | bytes 10223616 | tf_op jit(solution)/shard_map/dot_general | solution.py:33
  287.4 29.6 %all_to_all.63 = bf16[2,1,1536,384]{2,3,1,0:T(8,128)(2,1)S(1)} all-to-all(bf16[2,1,1536,384]{2,3,1,0:T(8,128)(2,1)S(1)} %bitcast.83), channel_id=1, replica_groups=mesh['expert'=64,'pair'=2,'dp'=2] {'dp'}, dimensions={0} | all-to-all | bytes 4718592 | tf_op jit(solution)/shard_map/all_to_all | solution.py:21
  318.8 6.9 %fusion.42 = f32[4,196,768]{2,1,0:T(8,128)} fusion(f32[4,196,128]{2,1,0:T(8,128)} %fusion.37, f32[4,196,128]{2,1,0:T(8,128)} %fusion.39, bf16[768,128]{1,0:T(8,128)(2,1)} %param.7, f32[4,196,128]{2,1,0:T(8,128)} %get-tuple-element.19, f32[4,196]{1,0:T(4,128)S(1)} %copy-done.6), kind=kOutput, calls=%fused_computation.48 | convolution fusion | flops 154844048 | bytes 3812416 | tf_op jit(solution)/shard_map/bms,ds->bmd/dot_general | solution.py:101
  325.8 3.5 add_convert_fusion
  329.3 2.8 copy.48
  332.1 130.2 %all-reduce.5.cloned.1.call-done = f32[768,128]{0,1:T(8,128)} async-done(((f32[768,128]{0,1:T(8,128)}), f32[768,128]{0,1:T(8,128)}) %all-reduce.5.cloned.1.call-update) | async-done | bytes 393232 | tf_op jit(solution)/shard_map/psum | solution.py:104
  464.2 42.7 %reduce-scatter.2.cloned.1.call-done = bf16[1,384,1536]{2,1,0:T(8,128)(2,1)} async-done(((bf16[1,768,1536]{2,1,0:T(8,128)(2,1)}), bf16[1,384,1536]{2,1,0:T(8,128)(2,1)}) %reduce-scatter.2.cloned.1.call-update) | async-done | bytes 1179664 | tf_op jit(solution)/shard_map/reduce_scatter | solution.py:81
  (49 shorter events, 30.1 us)
Async XLA Ops:
  7.2 86.9 %copy-start = (bf16[1,768,1536]{2,1,0:T(8,128)(2,1)S(1)}, bf16[1,768,1536]{2,1,0:T(8,128)(2,1)}, u32[]{:S(2)}) copy-start(bf16[1,768,1536]{2,1,0:T(8,128)(2,1)} %param.8) | copy-start | bytes 7077892
  9.1 44.6 %copy-start.4 = (f32[4,196,128]{2,1,0:T(8,128)}, f32[4,196,128]{2,1,0:T(8,128)S(1)}, u32[]{:S(2)}) copy-start(f32[4,196,128]{2,1,0:T(8,128)S(1)} %fusion.46) | copy-start | bytes 1204228
  10.0 0.6 copy-start.7
  16.8 35.9 %all-to-all-start.1 = ((bf16[4,64,2,768]{3,2,0,1:T(2,128)(2,1)}), bf16[4,64,2,768]{3,2,0,1:T(2,128)(2,1)S(1)}, u32[]{:S(2)}, u32[]{:S(2)}) async-start(bf16[4,64,2,768]{3,2,0,1:T(2,128)(2,1)} %copy.36), calls=%async_computation.1 | async-start | bytes 1572864 | tf_op jit(solution)/shard_map/all_to_all | solution.py:66
  29.8 59.6 %all-gather.5.cloned.1.call-start = ((), (), s32[]{:S(2)}) async-start(), calls=%async_computation.7 | async-start | bytes 2359296 | tf_op jit(solution)/shard_map/all_gather | solution.py:70
  52.7 0.9 copy-start.1
  53.7 65.0 %all-gather.3.cloned.1.call-start = ((), (), s32[]{:S(2)}) async-start(), calls=%async_computation.6 | async-start | bytes 2359296 | tf_op jit(solution)/shard_map/all_gather | solution.py:71
  184.6 34.6 %all-to-all-start.3 = ((bf16[256,1,2,768]{3,2,1,0:T(2,128)(2,1)}), bf16[256,1,2,768]{3,2,1,0:T(2,128)(2,1)S(1)}, u32[]{:S(2)}, u32[]{:S(2)}) async-start(bf16[256,1,2,768]{3,2,1,0:T(2,128)(2,1)} %copy.41), calls=%async_computation.3 | async-start | bytes 1572864 | tf_op jit(solution)/shard_map/all_to_all | solution.py:88
  196.3 78.5 %all-reduce.3.cloned.1.call-start = ((), (), s32[]{:S(2)}) async-start(), calls=%async_computation.8 | async-start | bytes 786432 | tf_op jit(solution)/shard_map/psum | solution.py:104
  220.6 4.4 copy-start.5
  222.9 3.0 copy-start.2
  223.0 2.1 copy-start.8
  232.8 229.5 %all-reduce.5.cloned.1.call-start = ((), (), s32[]{:S(2)}) async-start(), calls=%async_computation.9 | async-start | bytes 786432 | tf_op jit(solution)/shard_map/psum | solution.py:104
  274.8 232.1 %reduce-scatter.2.cloned.1.call-start = ((), (), s32[]{:S(2)}) async-start(), calls=%async_computation.10 | async-start | bytes 3538944 | tf_op jit(solution)/shard_map/reduce_scatter | solution.py:81
  317.0 1.8 copy-start.6
  317.4 8.4 %copy-start.9 = (f32[4,128]{1,0:T(4,128)S(1)}, f32[4,128]{1,0:T(4,128)}, u32[]{:S(2)}) copy-start(f32[4,128]{1,0:T(4,128)} %copy-done.7) | copy-start | bytes 6148
  318.8 6.9 %copy-start.3 = (bf16[4,128,768]{2,1,0:T(8,128)(2,1)S(1)}, bf16[4,128,768]{2,1,0:T(8,128)(2,1)}, u32[]{:S(2)}) copy-start(bf16[4,128,768]{2,1,0:T(8,128)(2,1)} %copy-done.2) | copy-start | bytes 2359300
Sparse Core Ops, SparseCore 0:
  53.8 29.1 all-gather.4
  89.5 29.1 all-gather.2
  232.9 41.8 all-reduce.2
  278.1 184.1 all-reduce.4
  465.2 41.6 reduce-scatter.1
